TPU v7x, 32 devices: a whole 2x2x4 slice. The times are simulated.
32 devices in a mesh: dom: 4 (over z), col: 8 (over y, x, core).
Axes of the slice: x: 2, y: 2, z: 4, core: 2. Of those that a mesh axis runs over, the one named last changes fastest.
Arguments:
- rhs_interior: bfloat16 [4, 48, 8192], P('dom', 'col'), may hold values from -6 to 6
- interior_inv: bfloat16 [4, 8192, 8192], P('dom', None, 'col'), may hold values from -0.0625 to 0.0625
- coupling: bfloat16 [4, 8192, 768], P('dom', 'col'), may hold values from -0.0625 to 0.0625
- rhs_interface: bfloat16 [48, 8192], P('col', 'dom'), may hold values from -6 to 6
- block_ids: int32 [4, 6], P('dom'), may hold values from 0 to 63, as said below
- interface_inv: bfloat16 [8192, 8192], P('dom', 'col'), may hold values from -0.0625 to 0.0625
Outputs:
- interior_solution: bfloat16 [4, 48, 8192], P('dom', None, 'col')
- interface_solution: bfloat16 [48, 8192], P('col')
Inputs may be any that keep to these rules, and one draw needn't show every extreme that they name: `block_ids`: each row names 6 different blocks.
All inputs are finite; a program needn't handle non-finite values.
Results may differ from a plain program's by a relative error of at most 0.025.
Values may be sent and summed in bfloat16 or wider, within the bound.
No kernel may reach another device: no remote copies, remote signals or barrier semaphores. Data moves between devices by JAX's collectives and lax.ppermute only.
A program may use at most 64 MiB of HBM per device.

v0:
```python
import jax
import jax.numpy as jnp
from jax import lax
from jax.sharding import PartitionSpec as P

G = 8192
BS = 128


def per_device(rhs_interior, interior_inv, coupling, rhs_interface, block_ids, interface_inv):
    rhs_local = rhs_interior[0]
    inverse = interior_inv[0]
    couple = coupling[0]
    blocks = block_ids[0]
    row_count = rhs_local.shape[0]
    block_count = blocks.shape[0]
    nblocks = G // BS
    onehot = (blocks[:, None] == jnp.arange(nblocks, dtype=jnp.int32)[None, :]).astype(jnp.float32)
    interior_step = jnp.dot(
        lax.all_gather(rhs_local, "col", axis=0, tiled=True),
        inverse,
        preferred_element_type=jnp.float32,
    ).astype(jnp.bfloat16)
    contribution = lax.psum_scatter(
        jnp.dot(interior_step, couple, preferred_element_type=jnp.float32).astype(jnp.bfloat16),
        "col",
        scatter_dimension=0,
        tiled=True,
    ).astype(jnp.float32)
    placed = jnp.einsum(
        "kb,rks->rbs", onehot, contribution.reshape(row_count, block_count, BS)
    ).reshape(row_count, G)
    summed = lax.psum_scatter(
        placed.astype(jnp.bfloat16), "dom", scatter_dimension=1, tiled=True
    ).astype(jnp.float32)
    reduced = (rhs_interface.astype(jnp.float32) - summed).astype(jnp.bfloat16)
    partial_solution = jnp.dot(
        lax.all_gather(reduced, "col", axis=0, tiled=True),
        interface_inv,
        preferred_element_type=jnp.float32,
    )
    column_total = lax.psum(partial_solution.astype(jnp.bfloat16), "dom")
    solution = lax.all_to_all(column_total, "col", split_axis=0, concat_axis=1, tiled=True)
    local_solution = jnp.einsum(
        "kb,rbs->rks",
        onehot.astype(jnp.bfloat16),
        solution.reshape(row_count, nblocks, BS),
        preferred_element_type=jnp.float32,
    )
    local_solution = local_solution.reshape(row_count, block_count * BS).astype(jnp.bfloat16)
    every_solution = lax.all_gather(local_solution, "col", axis=0, tiled=True)
    correction = jnp.einsum("rl,il->ri", every_solution, couple, preferred_element_type=jnp.float32)
    rhs_columns = lax.all_to_all(rhs_local, "col", split_axis=1, concat_axis=0, tiled=True)
    interior_rhs = (rhs_columns.astype(jnp.float32) - correction).astype(jnp.bfloat16)
    result = jnp.dot(
        lax.all_gather(interior_rhs, "col", axis=1, tiled=True),
        inverse,
        preferred_element_type=jnp.float32,
    )
    interior_solution = result.astype(jnp.bfloat16)[None]
    return (interior_solution, solution)


def solution(mesh):
    placed = (
        P("dom", "col", None),
        P("dom", None, "col"),
        P("dom", "col", None),
        P("col", "dom"),
        P("dom", None),
        P("dom", "col"),
    )
    return jax.shard_map(
        per_device,
        mesh=mesh,
        in_specs=placed,
        out_specs=(P("dom", None, "col"), P("col", None)),
        check_vma=False,
    )
```

profile of v0, /device:TPU:0, one launch (start us, length us, event | category | flops | bytes accessed | tf_op | source)
XLA Modules:
  0.0 168.0 jit_solution(9237124908893844768)
XLA Ops:
  7.2 0.0 copy-start
  7.2 0.0 reduce-scatter.4.cloned.1.call-start
  7.2 1.2 copy.15
  8.4 14.6 %all-gather = bf16[1,48,8192]{2,0,1:T(2,128)(2,1)S(1)} all-gather(bf16[1,6,8192]{2,0,1:T(2,128)(2,1)S(1)} %copy.15), channel_id=2, replica_groups=mesh['dom'=4,'col'=8] {'col'}, dimensions={1}, use_global_device_ids=true | all-gather | bytes 884736 | tf_op jit(solution)/shard_map/all_gather | solution.py:20
  23.0 0.0 copy-done
  23.0 0.0 copy-start.3
  23.0 0.0 copy-start.4
  23.0 0.0 copy-start.2
  23.0 9.5 %fusion.21 = bf16[48,768]{1,0:T(8,128)(2,1)S(1)} fusion(bf16[1,1024,768]{2,1,0:T(8,128)(2,1)S(1)} %copy-done, bf16[1,8192,1024]{2,1,0:T(8,128)(2,1)} %param.7, bf16[1,48,8192]{2,0,1:T(2,128)(2,1)S(1)} %all-gather), kind=kOutput, calls=%fused_computation.14 | convolution fusion | flops 880889856 | bytes 19210240 | tf_op jit(solution)/shard_map/dot_general | solution.py:25
  32.6 0.0 copy-start.1
  32.6 14.5 %fusion = bf16[8,768]{1,0:T(8,128)(2,1)S(1)} fusion(bf16[48,768]{1,0:T(8,128)(2,1)S(1)} %fusion.21), kind=kCustom, calls=%all-reduce-scatter | all-reduce-scatter fusion | flops 49153 | bytes 86528
  47.1 1.3 collective-permute-start
  48.4 2.0 %collective-permute-start.1 = (bf16[6,768]{1,0:T(8,128)(2,1)S(1)}, bf16[6,768]{1,0:T(8,128)(2,1)S(1)}, u32[]{:S(2)}, u32[]{:S(2)}) collective-permute-start(bf16[6,768]{1,0:T(8,128)(2,1)S(1)} %slice), channel_id=1, source_target_pairs={{0,2},{1,3},{2,4},{3,5},{4,6},{5,7},{8,10},{9,11},{10,12},{11,13},... | collective-permute-start | bytes 27656
  50.4 0.0 copy-done.3
  50.4 0.6 dynamic-slice.4
  51.7 0.1 collective-permute-done.1
  51.8 0.0 collective-permute-done
  51.8 0.2 concatenate
  52.1 0.0 copy-done.4
  52.1 0.3 fusion.24
  52.4 0.7 copy.25
  53.1 0.0 reduce-scatter.4.cloned.1.call-update
  53.1 0.0 all-reduce.4.cloned.1.call-start
  53.2 23.2 %reduce-scatter.4.cloned.1.call-done = bf16[6,2048]{1,0:T(8,128)(2,1)} async-done(((bf16[6,8192]{1,0:T(8,128)(2,1)}), bf16[6,2048]{1,0:T(8,128)(2,1)}) %reduce-scatter.4.cloned.1.call-update) | async-done | bytes 24592 | tf_op jit(solution)/shard_map/reduce_scatter | solution.py:33
  76.4 0.0 copy-done.2
  76.4 0.8 fusion.35
  77.1 9.3 %all-gather.1 = bf16[8,6,2048]{2,1,0:T(8,128)(2,1)S(1)} all-gather(bf16[1,6,2048]{2,1,0:T(8,128)(2,1)S(1)} %fusion.35), channel_id=1, replica_groups=mesh['dom'=4,'col'=8] {'col'}, dimensions={0}, use_global_device_ids=true | all-gather | bytes 221184 | tf_op jit(solution)/shard_map/all_gather | solution.py:38
  86.4 0.1 reshape.30
  86.5 3.0 %convolution_convert_fusion = bf16[48,1024]{1,0:T(8,128)(2,1)S(1)} fusion(bf16[48,2048]{1,0:T(8,128)(2,1)S(1)} %reshape.30, bf16[2048,1024]{1,0:T(8,128)(2,1)} %param.11), kind=kOutput, calls=%fused_computation.12 | convolution fusion | flops 201375744 | bytes 4489216 | tf_op jit(solution)/shard_map/dot_general | solution.py:37
  89.5 0.7 all_to_all.26
  90.2 0.0 all-reduce.4.cloned.1.call-update
  90.2 0.0 copy-done.1
  90.2 8.0 %all_to_all.32 = bf16[6,8,1024]{2,0,1:T(8,128)(2,1)S(1)} all-to-all(bf16[6,8,1024]{2,0,1:T(8,128)(2,1)S(1)} %bitcast.65), channel_id=1, replica_groups=mesh['dom'=4,'col'=8] {'col'}, dimensions={1} | all-to-all | bytes 196608 | tf_op jit(solution)/shard_map/all_to_all | solution.py:53
  98.3 24.0 %all-reduce.4.cloned.1.call-done = bf16[8,6,1024]{2,1,0:T(8,128)(2,1)} async-done(((bf16[8,6,1024]{2,1,0:T(8,128)(2,1)}), bf16[8,6,1024]{2,1,0:T(8,128)(2,1)}) %all-reduce.4.cloned.1.call-update) | async-done | bytes 98320 | tf_op jit(solution)/shard_map/psum | solution.py:42
  122.3 3.6 %all-to-all-start.1 = ((bf16[8,6,1024]{2,1,0:T(8,128)(2,1)}), bf16[8,6,1024]{2,1,0:T(8,128)(2,1)S(1)}, u32[]{:S(2)}, u32[]{:S(2)}) async-start(bf16[8,6,1024]{2,1,0:T(8,128)(2,1)} %all-reduce.4.cloned.1.call-done), calls=%async_computation.2 | async-start | bytes 262144 | tf_op jit(solution)/shard_map/all_to_all | solution.py:43
  126.0 5.4 %all-to-all-done.1 = bf16[8,6,1024]{2,1,0:T(8,128)(2,1)S(1)} async-done(((bf16[8,6,1024]{2,1,0:T(8,128)(2,1)}), bf16[8,6,1024]{2,1,0:T(8,128)(2,1)S(1)}, u32[]{:S(2)}, u32[]{:S(2)}) %all-to-all-start.1) | async-done | bytes 98336 | tf_op jit(solution)/shard_map/all_to_all | solution.py:43
  131.4 0.1 copy.16
  131.5 0.2 fusion.28
  131.7 8.3 %all-gather.2 = bf16[8,6,768]{2,1,0:T(8,128)(2,1)S(1)} all-gather(bf16[1,6,768]{2,1,0:T(8,128)(2,1)S(1)} %reshape.31), channel_id=1, replica_groups=mesh['dom'=4,'col'=8] {'col'}, dimensions={0}, use_global_device_ids=true | all-gather | bytes 82944 | tf_op jit(solution)/shard_map/all_gather | solution.py:51
  140.1 0.6 fusion.12
  140.6 10.4 %all_gather.15 = bf16[48,8192]{1,0:T(8,128)(2,1)S(1)} all-gather(bf16[48,1024]{1,0:T(8,128)(2,1)S(1)} %fusion.12), channel_id=1, replica_groups=mesh['dom'=4,'col'=8] {'col'}, dimensions={1}, use_global_device_ids=true | all-gather | bytes 884736 | tf_op jit(solution)/shard_map/all_gather | solution.py:56
  151.0 9.5 %fusion.25 = bf16[1,48,1024]{2,1,0:T(8,128)(2,1)} fusion(bf16[48,8192]{1,0:T(8,128)(2,1)S(1)} %all_gather.15, bf16[1,8192,1024]{2,1,0:T(8,128)(2,1)} %param.7), kind=kOutput, calls=%fused_computation.16 | convolution fusion | flops 805355520 | bytes 17661952 | tf_op jit(solution)/shard_map/dot_general | solution.py:55
  160.5 0.7 copy.28
  (8 shorter events, 0.2 us)
Async XLA Ops:
  7.2 15.9 %copy-start = (bf16[1,1024,768]{2,1,0:T(8,128)(2,1)S(1)}, bf16[1,1024,768]{2,1,0:T(8,128)(2,1)}, u32[]{:S(2)}) copy-start(bf16[1,1024,768]{2,1,0:T(8,128)(2,1)} %param.8) | copy-start | bytes 4718596
  7.2 69.2 %reduce-scatter.4.cloned.1.call-start = ((), (), s32[]{:S(2)}) async-start(), calls=%async_computation.3 | async-start | bytes 163840 | tf_op jit(solution)/shard_map/reduce_scatter | solution.py:33
  23.0 27.4 %copy-start.3 = (u32[32]{0:T(128)S(1)}, u32[32]{0:T(128)}, u32[]{:S(2)}) copy-start(u32[32]{0:T(128)} %constant.7) | copy-start | bytes 388
  23.0 29.0 %copy-start.4 = (s32[1,6]{1,0:T(1,128)S(1)}, s32[1,6]{1,0:T(1,128)}, u32[]{:S(2)}) copy-start(s32[1,6]{1,0:T(1,128)} %param.10) | copy-start | bytes 76
  23.0 53.3 %copy-start.2 = (bf16[6,2048]{1,0:T(8,128)(2,1)S(1)}, bf16[6,2048]{1,0:T(8,128)(2,1)}, u32[]{:S(2)}) copy-start(bf16[6,2048]{1,0:T(8,128)(2,1)} %param.9) | copy-start | bytes 73732
  32.6 57.6 %copy-start.1 = (bf16[1,6,8192]{2,1,0:T(8,128)(2,1)S(1)}, bf16[1,6,8192]{2,1,0:T(8,128)(2,1)}, u32[]{:S(2)}) copy-start(bf16[1,6,8192]{2,1,0:T(8,128)(2,1)} %param.6) | copy-start | bytes 294916
  47.1 4.7 %collective-permute-start = (bf16[8,768]{1,0:T(8,128)(2,1)S(1)}, bf16[8,768]{1,0:T(8,128)(2,1)S(1)}, u32[]{:S(2)}, u32[]{:S(2)}) collective-permute-start(bf16[8,768]{1,0:T(8,128)(2,1)S(1)} %fusion), channel_id=1, source_target_pairs={{0,1},{1,2},{2,3},{3,4},{4,5},{5,6},{6,7},{8,9},{9,10},{10,11},{11... | collective-permute-start | bytes 36872
  48.4 3.4 %collective-permute-start.1 = (bf16[6,768]{1,0:T(8,128)(2,1)S(1)}, bf16[6,768]{1,0:T(8,128)(2,1)S(1)}, u32[]{:S(2)}, u32[]{:S(2)}) collective-permute-start(bf16[6,768]{1,0:T(8,128)(2,1)S(1)} %slice), channel_id=1, source_target_pairs={{0,2},{1,3},{2,4},{3,5},{4,6},{5,7},{8,10},{9,11},{10,12},{11,13},... | collective-permute-start | bytes 27656
  53.1 69.1 %all-reduce.4.cloned.1.call-start = ((), (), s32[]{:S(2)}) async-start(), calls=%async_computation.4 | async-start | bytes 262144 | tf_op jit(solution)/shard_map/psum | solution.py:42
  122.3 9.1 %all-to-all-start.1 = ((bf16[8,6,1024]{2,1,0:T(8,128)(2,1)}), bf16[8,6,1024]{2,1,0:T(8,128)(2,1)S(1)}, u32[]{:S(2)}, u32[]{:S(2)}) async-start(bf16[8,6,1024]{2,1,0:T(8,128)(2,1)} %all-reduce.4.cloned.1.call-done), calls=%async_computation.2 | async-start | bytes 262144 | tf_op jit(solution)/shard_map/all_to_all | solution.py:43
Sparse Core Ops, SparseCore 0:
  53.3 23.0 reduce-scatter.3
  90.3 31.8 all-reduce.3
where the time goes:
time: 169 us; the launch traced here: 168 us
  blocking collectives  65 us (38%)
  waiting for transfers between devices  52.8 us (31%)
  matrix products  23.1 us (14%)
  between operations  14.9 us (9%)
  starting transfers between devices  7.03 us (4%)
  local copies, waits for them, and re-layouts  4.39 us (3%)
    psum x1, waiting for transfers between devices, per_device(): column_total = lax.psum(partial_solution.astype(jnp.bfloat16), 'dom')  24 us
    reduce_scatter x1, waiting for transfers between devices, per_device(): lax.psum_scatter(placed.astype(jnp.bfloat16), 'dom', scatter_dimension=1,...  23.2 us
    all_gather x1, blocking collectives, per_device(): lax.all_gather(rhs_local, 'col', axis=0, tiled=True)  14.6 us
    unnamed x1, blocking collectives  14.5 us
    all_gather x1, blocking collectives, per_device(): lax.all_gather(interior_rhs, 'col', axis=1, tiled=True)  10.4 us
    dot_general x1, matrix products, per_device(): jnp.dot(interior_step, couple, preferred_element_type=jnp.float32)  9.54 us
    dot_general x1, matrix products, per_device(): jnp.dot(lax.all_gather(interior_rhs, 'col', axis=1, tiled=True), inverse,...  9.46 us
    all_gather x1, blocking collectives, per_device(): lax.all_gather(reduced, 'col', axis=0, tiled=True)  9.25 us
  transfers between devices with their start and end apart: 5, of which 4 were waited for; matrix products, arithmetic and copies ran while one was open for 0% of the time, Pallas kernels for 0%

commit v1 on v0

--- a/solution.py
+++ b/solution.py
@@ -39,7 +39,7 @@
         interface_inv,
         preferred_element_type=jnp.float32,
     )
-    column_total = lax.psum(partial_solution.astype(jnp.bfloat16), "dom")
+    column_total = jnp.sum(lax.all_gather(partial_solution.astype(jnp.bfloat16), "dom"), axis=0)
     solution = lax.all_to_all(column_total, "col", split_axis=0, concat_axis=1, tiled=True)
     local_solution = jnp.einsum(
         "kb,rbs->rks",

time: 169 us -> 151 us (0.89)
  waiting for transfers between devices: 52.8 us -> 22.6 us
  blocking collectives: 65 us -> 72.2 us
  starting transfers between devices: 7.03 us -> 12.8 us
    psum x1 -> x0, waiting for transfers between devices: 24 us -> none  [per_device(): column_total = lax.psum(partial_solution.astype(jnp.bfloat16), 'dom')]
    all_gather x0 -> x1, blocking collectives: none -> 15.4 us  [per_device(): lax.all_gather(partial_solution.astype(jnp.bfloat16), 'dom')]
    all_to_all x1 -> x0, blocking collectives: 8.04 us -> none  [per_device(): lax.all_to_all(rhs_local, 'col', split_axis=1, concat_axis=0, tiled=True)]
    all_to_all x0 -> x1, starting transfers between devices: none -> 6.11 us  [per_device(): lax.all_to_all(rhs_local, 'col', split_axis=1, concat_axis=0, tiled=True)]
    reduce_scatter x1, waiting for transfers between devices: 23.2 us -> 17.1 us  [per_device(): lax.psum_scatter(placed.astype(jnp.bfloat16), 'dom', scatter_dimension=1,...]
    unnamed x20 -> x18, local copies, waits for them, and re-layouts: 3.53 us -> 3.52 us
  transfers between devices with their start and end apart: 5 -> 5, of which waited for: 4 -> 3; matrix products, arithmetic and copies ran while one was open for 0% -> 3% of each run, Pallas kernels for 0% -> 0%
where the time goes in v1:
time: 151 us
  blocking collectives  72.2 us (48%)
  matrix products  23.1 us (15%)
  waiting for transfers between devices  22.6 us (15%)
  between operations  14.8 us (10%)
  starting transfers between devices  12.8 us (8%)
  local copies, waits for them, and re-layouts  4.38 us (3%)
    reduce_scatter x1, waiting for transfers between devices, per_device(): lax.psum_scatter(placed.astype(jnp.bfloat16), 'dom', scatter_dimension=1,...  17.1 us
    all_gather x1, blocking collectives, per_device(): lax.all_gather(partial_solution.astype(jnp.bfloat16), 'dom')  15.4 us
    all_gather x1, blocking collectives, per_device(): lax.all_gather(rhs_local, 'col', axis=0, tiled=True)  14.6 us
    unnamed x1, blocking collectives  14.3 us
    all_gather x1, blocking collectives, per_device(): lax.all_gather(interior_rhs, 'col', axis=1, tiled=True)  10.4 us
    dot_general x1, matrix products, per_device(): jnp.dot(interior_step, couple, preferred_element_type=jnp.float32)  9.54 us
    dot_general x1, matrix products, per_device(): jnp.dot(lax.all_gather(interior_rhs, 'col', axis=1, tiled=True), inverse,...  9.46 us
    all_gather x1, blocking collectives, per_device(): lax.all_gather(reduced, 'col', axis=0, tiled=True)  9.25 us
  transfers between devices with their start and end apart: 5, of which 3 were waited for; matrix products, arithmetic and copies ran while one was open for 3% of the time, Pallas kernels for 0%

profile of v1, /device:TPU:0, one launch (start us, length us, event | category | flops | bytes accessed | tf_op | source)
XLA Modules:
  0.0 150.8 jit_solution(17846333750220462374)
XLA Ops:
  7.2 0.0 copy-start
  7.2 0.0 reduce-scatter.4.cloned.1.call-start
  7.2 1.2 copy.14
  8.4 14.6 %all-gather = bf16[1,48,8192]{2,0,1:T(2,128)(2,1)S(1)} all-gather(bf16[1,6,8192]{2,0,1:T(2,128)(2,1)S(1)} %copy.14), channel_id=2, replica_groups=mesh['dom'=4,'col'=8] {'col'}, dimensions={1}, use_global_device_ids=true | all-gather | bytes 884736 | tf_op jit(solution)/shard_map/all_gather | solution.py:20
  23.0 0.0 copy-done
  23.0 0.0 copy-start.2
  23.0 0.0 copy-start.3
  23.0 0.0 copy-start.1
  23.0 9.5 %fusion.21 = bf16[48,768]{1,0:T(8,128)(2,1)S(1)} fusion(bf16[1,1024,768]{2,1,0:T(8,128)(2,1)S(1)} %copy-done, bf16[1,8192,1024]{2,1,0:T(8,128)(2,1)} %param.7, bf16[1,48,8192]{2,0,1:T(2,128)(2,1)S(1)} %all-gather), kind=kOutput, calls=%fused_computation.14 | convolution fusion | flops 880889856 | bytes 19210240 | tf_op jit(solution)/shard_map/dot_general | solution.py:25
  32.6 14.3 %fusion = bf16[8,768]{1,0:T(8,128)(2,1)S(1)} fusion(bf16[48,768]{1,0:T(8,128)(2,1)S(1)} %fusion.21), kind=kCustom, calls=%all-reduce-scatter | all-reduce-scatter fusion | flops 49153 | bytes 86528
  46.9 1.3 collective-permute-start
  48.2 2.0 %collective-permute-start.1 = (bf16[6,768]{1,0:T(8,128)(2,1)S(1)}, bf16[6,768]{1,0:T(8,128)(2,1)S(1)}, u32[]{:S(2)}, u32[]{:S(2)}) collective-permute-start(bf16[6,768]{1,0:T(8,128)(2,1)S(1)} %slice), channel_id=1, source_target_pairs={{0,2},{1,3},{2,4},{3,5},{4,6},{5,7},{8,10},{9,11},{10,12},{11,13},... | collective-permute-start | bytes 27656
  50.3 0.0 copy-done.2
  50.3 0.6 dynamic-slice.4
  51.5 0.1 collective-permute-done.1
  51.7 0.0 collective-permute-done
  51.7 0.2 concatenate
  51.9 0.0 copy-done.3
  51.9 0.3 fusion.24
  52.2 0.7 copy.24
  53.0 0.0 reduce-scatter.4.cloned.1.call-update
  53.0 6.1 %all-to-all-start = ((bf16[6,8,1024]{2,0,1:T(8,128)(2,1)}), bf16[6,8,1024]{2,0,1:T(8,128)(2,1)S(1)}, u32[]{:S(2)}, u32[]{:S(2)}) async-start(bf16[6,8,1024]{2,0,1:T(8,128)(2,1)} %bitcast), calls=%async_computation | async-start | bytes 262144 | tf_op jit(solution)/shard_map/all_to_all | solution.py:53
  59.1 17.1 %reduce-scatter.4.cloned.1.call-done = bf16[6,2048]{1,0:T(8,128)(2,1)} async-done(((bf16[6,8192]{1,0:T(8,128)(2,1)}), bf16[6,2048]{1,0:T(8,128)(2,1)}) %reduce-scatter.4.cloned.1.call-update) | async-done | bytes 24592 | tf_op jit(solution)/shard_map/reduce_scatter | solution.py:33
  76.2 0.0 copy-done.1
  76.2 0.8 fusion.35
  77.0 9.3 %all-gather.2 = bf16[8,6,2048]{2,1,0:T(8,128)(2,1)S(1)} all-gather(bf16[1,6,2048]{2,1,0:T(8,128)(2,1)S(1)} %fusion.35), channel_id=1, replica_groups=mesh['dom'=4,'col'=8] {'col'}, dimensions={0}, use_global_device_ids=true | all-gather | bytes 221184 | tf_op jit(solution)/shard_map/all_gather | solution.py:38
  86.2 0.1 reshape.31
  86.3 3.0 %convolution_convert_fusion = bf16[48,1024]{1,0:T(8,128)(2,1)S(1)} fusion(bf16[48,2048]{1,0:T(8,128)(2,1)S(1)} %reshape.31, bf16[2048,1024]{1,0:T(8,128)(2,1)} %param.11), kind=kOutput, calls=%fused_computation.12 | convolution fusion | flops 201375744 | bytes 4489216 | tf_op jit(solution)/shard_map/dot_general | solution.py:37
  89.3 15.4 %all-gather.1 = bf16[192,1024]{1,0:T(8,128)(2,1)S(1)} all-gather(bf16[48,1024]{1,0:T(8,128)(2,1)S(1)} %convolution_convert_fusion), channel_id=3, replica_groups=mesh['dom'=4,'col'=8] {'dom'}, dimensions={0}, use_global_device_ids=true | all-gather | bytes 491520 | tf_op jit(solution)/shard_map/all_gather | solution.py:42
  104.7 0.1 reduce_sum.12
  104.8 0.7 all_to_all.26
  105.5 0.0 all-to-all-done
  105.5 3.4 %all-to-all-start.1 = ((bf16[8,6,1024]{2,1,0:T(8,128)(2,1)}), bf16[8,6,1024]{2,1,0:T(8,128)(2,1)S(1)}, u32[]{:S(2)}, u32[]{:S(2)}) async-start(bf16[8,6,1024]{2,1,0:T(8,128)(2,1)} %all_to_all.26), calls=%async_computation.2 | async-start | bytes 262144 | tf_op jit(solution)/shard_map/all_to_all | solution.py:43
  108.9 5.4 %all-to-all-done.1 = bf16[8,6,1024]{2,1,0:T(8,128)(2,1)S(1)} async-done(((bf16[8,6,1024]{2,1,0:T(8,128)(2,1)}), bf16[8,6,1024]{2,1,0:T(8,128)(2,1)S(1)}, u32[]{:S(2)}, u32[]{:S(2)}) %all-to-all-start.1) | async-done | bytes 98336 | tf_op jit(solution)/shard_map/all_to_all | solution.py:43
  114.3 0.1 copy.15
  114.4 0.2 fusion.28
  114.6 8.3 %all-gather.3 = bf16[8,6,768]{2,1,0:T(8,128)(2,1)S(1)} all-gather(bf16[1,6,768]{2,1,0:T(8,128)(2,1)S(1)} %reshape.32), channel_id=1, replica_groups=mesh['dom'=4,'col'=8] {'col'}, dimensions={0}, use_global_device_ids=true | all-gather | bytes 82944 | tf_op jit(solution)/shard_map/all_gather | solution.py:51
  122.9 0.6 fusion.12
  123.5 10.4 %all_gather.23 = bf16[48,8192]{1,0:T(8,128)(2,1)S(1)} all-gather(bf16[48,1024]{1,0:T(8,128)(2,1)S(1)} %fusion.12), channel_id=1, replica_groups=mesh['dom'=4,'col'=8] {'col'}, dimensions={1}, use_global_device_ids=true | all-gather | bytes 884736 | tf_op jit(solution)/shard_map/all_gather | solution.py:56
  133.9 9.5 %fusion.25 = bf16[1,48,1024]{2,1,0:T(8,128)(2,1)} fusion(bf16[48,8192]{1,0:T(8,128)(2,1)S(1)} %all_gather.23, bf16[1,8192,1024]{2,1,0:T(8,128)(2,1)} %param.7), kind=kOutput, calls=%fused_computation.16 | convolution fusion | flops 805355520 | bytes 17661952 | tf_op jit(solution)/shard_map/dot_general | solution.py:55
  143.3 0.7 copy.26
  (8 shorter events, 0.2 us)
Async XLA Ops:
  7.2 15.9 %copy-start = (bf16[1,1024,768]{2,1,0:T(8,128)(2,1)S(1)}, bf16[1,1024,768]{2,1,0:T(8,128)(2,1)}, u32[]{:S(2)}) copy-start(bf16[1,1024,768]{2,1,0:T(8,128)(2,1)} %param.8) | copy-start | bytes 4718596
  7.2 69.0 %reduce-scatter.4.cloned.1.call-start = ((), (), s32[]{:S(2)}) async-start(), calls=%async_computation.3 | async-start | bytes 163840 | tf_op jit(solution)/shard_map/reduce_scatter | solution.py:33
  23.0 27.2 %copy-start.2 = (u32[32]{0:T(128)S(1)}, u32[32]{0:T(128)}, u32[]{:S(2)}) copy-start(u32[32]{0:T(128)} %constant.10) | copy-start | bytes 388
  23.0 28.9 %copy-start.3 = (s32[1,6]{1,0:T(1,128)S(1)}, s32[1,6]{1,0:T(1,128)}, u32[]{:S(2)}) copy-start(s32[1,6]{1,0:T(1,128)} %param.10) | copy-start | bytes 76
  23.0 53.2 %copy-start.1 = (bf16[6,2048]{1,0:T(8,128)(2,1)S(1)}, bf16[6,2048]{1,0:T(8,128)(2,1)}, u32[]{:S(2)}) copy-start(bf16[6,2048]{1,0:T(8,128)(2,1)} %param.9) | copy-start | bytes 73732
  46.9 4.7 %collective-permute-start = (bf16[8,768]{1,0:T(8,128)(2,1)S(1)}, bf16[8,768]{1,0:T(8,128)(2,1)S(1)}, u32[]{:S(2)}, u32[]{:S(2)}) collective-permute-start(bf16[8,768]{1,0:T(8,128)(2,1)S(1)} %fusion), channel_id=1, source_target_pairs={{0,1},{1,2},{2,3},{3,4},{4,5},{5,6},{6,7},{8,9},{9,10},{10,11},{11... | collective-permute-start | bytes 36872
  48.2 3.4 %collective-permute-start.1 = (bf16[6,768]{1,0:T(8,128)(2,1)S(1)}, bf16[6,768]{1,0:T(8,128)(2,1)S(1)}, u32[]{:S(2)}, u32[]{:S(2)}) collective-permute-start(bf16[6,768]{1,0:T(8,128)(2,1)S(1)} %slice), channel_id=1, source_target_pairs={{0,2},{1,3},{2,4},{3,5},{4,6},{5,7},{8,10},{9,11},{10,12},{11,13},... | collective-permute-start | bytes 27656
  53.0 52.5 %all-to-all-start = ((bf16[6,8,1024]{2,0,1:T(8,128)(2,1)}), bf16[6,8,1024]{2,0,1:T(8,128)(2,1)S(1)}, u32[]{:S(2)}, u32[]{:S(2)}) async-start(bf16[6,8,1024]{2,0,1:T(8,128)(2,1)} %bitcast), calls=%async_computation | async-start | bytes 262144 | tf_op jit(solution)/shard_map/all_to_all | solution.py:53
  105.5 8.8 %all-to-all-start.1 = ((bf16[8,6,1024]{2,1,0:T(8,128)(2,1)}), bf16[8,6,1024]{2,1,0:T(8,128)(2,1)S(1)}, u32[]{:S(2)}, u32[]{:S(2)}) async-start(bf16[8,6,1024]{2,1,0:T(8,128)(2,1)} %all_to_all.26), calls=%async_computation.2 | async-start | bytes 262144 | tf_op jit(solution)/shard_map/all_to_all | solution.py:43
Sparse Core Ops, SparseCore 0:
  53.1 23.0 reduce-scatter.3
